TPU v7x, 32 devices: a whole 2x2x4 slice. The times are simulated.
32 devices in a mesh: real: 2 (over x), tile: 16 (over z, y, core).
Axes of the slice: x: 2, y: 2, z: 4, core: 2. Of those that a mesh axis runs over, the one named last changes fastest.
Arguments:
- positions: float32 [6, 8192], P('real', 'tile'), parts along dimension 0, may hold values from -1.5 to 125.5, as said below
- residual: float32 [6, 8192], P('real', 'tile'), parts along dimension 0, may hold values from -24 to 24
- iterate: float32 [6, 8192], P('real', 'tile'), parts along dimension 0, may hold values from -6 to 6
Outputs:
- new_iterate: float32 [6, 8192], P('real', 'tile'), parts along dimension 0
- new_residual: float32 [6, 8192], P('real', 'tile'), parts along dimension 0
- new_direction: float32 [6, 8192], P('real', 'tile'), parts along dimension 0
There are 2 independent parts, one for each index of `real`. A program takes and returns all parts, laid end to end along the dimension named above; each array names one. Nothing has to cross between parts.
Inputs may be any that keep to these rules, and one draw needn't show every extreme that they name: `positions`: distinct blobs are at least 1 apart.
All inputs are finite; a program needn't handle non-finite values.
Results may differ from a plain program's by a relative error of at most 0.0003.
Values sent between devices are 32-bit elements; how exact they have to be, the bound alone decides.
No kernel may reach another device: no remote copies, remote signals or barrier semaphores. Data moves between devices by JAX's collectives and lax.ppermute only.
A program may use at most 64 MiB of HBM per device.

v0:
```python
import jax
import jax.numpy as jnp
from jax import lax
from jax.sharding import PartitionSpec as P


def pair_terms(row_pos, col_pos):
    separation = row_pos[:, :, None] - col_pos[:, None, :]
    squared = jnp.sum(separation * separation, axis=0)
    radius = jnp.sqrt(squared)
    inverse = 1.0 / jnp.maximum(radius, 0.5)
    inverse_sq = inverse * inverse
    far_scalar = 0.75 * inverse * (1.0 + 2.0 / 3.0 * inverse_sq)
    far_tensor = 0.75 * (1.0 - 2.0 * inverse_sq) * inverse_sq * inverse
    touching = radius < 2.0
    scalar_part = jnp.where(touching, 1.0 - 9.0 / 32.0 * radius, far_scalar)
    tensor_part = jnp.where(touching, 3.0 / 32.0 * inverse, far_tensor)
    return (separation, scalar_part, tensor_part)


def toward_rows(separation, scalar_part, tensor_part, col_forces):
    projected = jnp.sum(separation * col_forces[:, None, :], axis=0)
    return jnp.sum(
        scalar_part[None] * col_forces[:, None, :] + (tensor_part * projected)[None] * separation,
        axis=2,
    )


def shards(positions, residual, iterate):
    own_blobs = positions.shape[1]
    old_norm = lax.psum(jnp.sum(residual * residual), "tile")
    col_pos = lax.all_gather(positions, "tile", axis=1, tiled=True)
    col_forces = lax.all_gather(residual, "tile", axis=1, tiled=True)
    portion_cols = col_pos.shape[1]
    col_block = portion_cols
    for factor in (4, 2, 1):
        col_block = factor * own_blobs
        break

    def add_block(turn_index, running):
        block_pos = lax.dynamic_slice_in_dim(col_pos, turn_index * col_block, col_block, 1)
        block_forces = lax.dynamic_slice_in_dim(col_forces, turn_index * col_block, col_block, 1)
        separation, scalar_part, tensor_part = pair_terms(positions, block_pos)
        return running + toward_rows(separation, scalar_part, tensor_part, block_forces)

    applied = lax.fori_loop(0, portion_cols // col_block, add_block, jnp.zeros_like(residual))
    curvature = lax.psum(jnp.sum(residual * applied), "tile")
    step_size = old_norm / curvature
    new_residual = residual - step_size * applied
    new_norm = lax.psum(jnp.sum(new_residual * new_residual), "tile")
    new_iterate = iterate + step_size * residual
    new_direction = new_residual + new_norm / old_norm * residual
    return (new_iterate, new_residual, new_direction)


def solution(mesh):
    return jax.shard_map(
        shards,
        mesh=mesh,
        in_specs=(P("real", "tile"), P("real", "tile"), P("real", "tile")),
        out_specs=(P("real", "tile"), P("real", "tile"), P("real", "tile")),
        check_vma=False,
    )
```

profile of v0, /device:TPU:0, one launch (start us, length us, event | category | flops | bytes accessed | tf_op | source)
XLA Modules:
  0.0 165.1 jit_solution(6442482215898881509)
XLA Ops:
  0.6 23.7 %all_gather.6 = f32[3,8192]{1,0:T(4,128)S(1)} all-gather(f32[3,512]{1,0:T(4,128)} %param.5), channel_id=1, replica_groups=mesh['real'=2,'tile'=16] {'tile'}, dimensions={1}, use_global_device_ids=true | all-gather | bytes 104448 | tf_op jit(solution)/shard_map/all_gather | solution.py:32
  24.3 18.0 %all_gather.7 = f32[3,8192]{1,0:T(4,128)S(1)} all-gather(f32[3,512]{1,0:T(4,128)} %param.6), channel_id=1, replica_groups=mesh['real'=2,'tile'=16] {'tile'}, dimensions={1}, use_global_device_ids=true | all-gather | bytes 104448 | tf_op jit(solution)/shard_map/all_gather | solution.py:33
  42.4 0.0 copy-start.1
  42.4 0.0 copy-start.3
  42.4 56.4 %while.14 = (s32[]{:T(128)}, f32[3,512]{1,0:T(4,128)S(1)}, f32[3,512]{1,0:T(4,128)}, f32[3,8192]{1,0:T(4,128)S(1)}, f32[3,8192]{1,0:T(4,128)S(1)}, /*index=5*/s32[]{:T(128)}, s32[]{:T(128)}, s32[]{:T(128)}, s32[]{:T(128)}) while((s32[]{:T(128)}, f32[3,512]{1,0:T(4,128)S(1)}, f32[3,512]{1,0:T(4,128)}, f32[3,8192]{1,0:T(4,128)S(1)}, ...), condition=%wide.region_6.7_spmd.clone, body=%wide.region_2.6_spmd.clone.sunk | while | flops 49284612 | bytes 33812656 | solution.py:46
  42.4 8.2 %fusion.10 = (f32[512,2048]{1,0:T(8,128)S(1)}, f32[512,2048]{1,0:T(8,128)S(1)}) fusion(f32[3,2048]{1,0:T(4,128)S(1)} %get-tuple-element.177, f32[3,512]{1,0:T(4,128)} %get-tuple-element.203, f32[3,2048]{1,0:T(4,128)S(1)} %get-tuple-element.178), kind=kLoop, calls=%fused_computation.3.clone.1 | loop fusion | flops 13631488 | bytes 8443904 | tf_op jit(solution)/shard_map/while/body/eval_jaxpr/reduce_sum | solution.py:9
  50.6 0.0 copy-start
  50.6 3.6 %fusion.11 = (f32[512,2048]{1,0:T(8,128)S(1)}, f32[512,2048]{1,0:T(8,128)S(1)}) fusion(f32[512,2048]{1,0:T(8,128)S(1)} %get-tuple-element.179, f32[512,2048]{1,0:T(8,128)S(1)} %get-tuple-element.180), kind=kLoop, calls=%fused_computation.11.clone.1 | loop fusion | flops 19922944 | bytes 16777216 | tf_op jit(solution)/shard_map/while/body/eval_jaxpr/jit(_where)/select_n | solution.py:16
  54.2 0.0 copy-done
  54.2 2.3 %fusion.12 = f32[3,512]{1,0:T(4,128)S(1)} fusion(f32[512,2048]{1,0:T(8,128)S(1)} %get-tuple-element.181, f32[3,2048]{1,0:T(4,128)S(1)} %get-tuple-element.178, f32[512,2048]{1,0:T(8,128)S(1)} %get-tuple-element.182, f32[3,2048]{1,0:T(4,128)S(1)} %get-tuple-element.177, f32[3,512]{1,0:T(4,128)S(1)} %copy-done), kind=kLoop, calls=%fused_computation.6.clone.1 | loop fusion | flops 15727104 | bytes 8450048 | tf_op jit(solution)/shard_map/while/body/eval_jaxpr/reduce_sum | solution.py:23
  56.5 8.2 %fusion.10 = (f32[512,2048]{1,0:T(8,128)S(1)}, f32[512,2048]{1,0:T(8,128)S(1)}) fusion(f32[3,2048]{1,0:T(4,128)S(1)} %get-tuple-element.177, f32[3,512]{1,0:T(4,128)} %get-tuple-element.203, f32[3,2048]{1,0:T(4,128)S(1)} %get-tuple-element.178), kind=kLoop, calls=%fused_computation.3.clone.1 | loop fusion | flops 13631488 | bytes 8443904 | tf_op jit(solution)/shard_map/while/body/eval_jaxpr/reduce_sum | solution.py:9
  64.7 0.0 copy-start
  64.7 3.6 %fusion.11 = (f32[512,2048]{1,0:T(8,128)S(1)}, f32[512,2048]{1,0:T(8,128)S(1)}) fusion(f32[512,2048]{1,0:T(8,128)S(1)} %get-tuple-element.179, f32[512,2048]{1,0:T(8,128)S(1)} %get-tuple-element.180), kind=kLoop, calls=%fused_computation.11.clone.1 | loop fusion | flops 19922944 | bytes 16777216 | tf_op jit(solution)/shard_map/while/body/eval_jaxpr/jit(_where)/select_n | solution.py:16
  68.3 0.0 copy-done
  68.3 2.3 %fusion.12 = f32[3,512]{1,0:T(4,128)S(1)} fusion(f32[512,2048]{1,0:T(8,128)S(1)} %get-tuple-element.181, f32[3,2048]{1,0:T(4,128)S(1)} %get-tuple-element.178, f32[512,2048]{1,0:T(8,128)S(1)} %get-tuple-element.182, f32[3,2048]{1,0:T(4,128)S(1)} %get-tuple-element.177, f32[3,512]{1,0:T(4,128)S(1)} %copy-done), kind=kLoop, calls=%fused_computation.6.clone.1 | loop fusion | flops 15727104 | bytes 8450048 | tf_op jit(solution)/shard_map/while/body/eval_jaxpr/reduce_sum | solution.py:23
  70.6 8.2 %fusion.10 = (f32[512,2048]{1,0:T(8,128)S(1)}, f32[512,2048]{1,0:T(8,128)S(1)}) fusion(f32[3,2048]{1,0:T(4,128)S(1)} %get-tuple-element.177, f32[3,512]{1,0:T(4,128)} %get-tuple-element.203, f32[3,2048]{1,0:T(4,128)S(1)} %get-tuple-element.178), kind=kLoop, calls=%fused_computation.3.clone.1 | loop fusion | flops 13631488 | bytes 8443904 | tf_op jit(solution)/shard_map/while/body/eval_jaxpr/reduce_sum | solution.py:9
  78.8 0.0 copy-start
  78.8 3.6 %fusion.11 = (f32[512,2048]{1,0:T(8,128)S(1)}, f32[512,2048]{1,0:T(8,128)S(1)}) fusion(f32[512,2048]{1,0:T(8,128)S(1)} %get-tuple-element.179, f32[512,2048]{1,0:T(8,128)S(1)} %get-tuple-element.180), kind=kLoop, calls=%fused_computation.11.clone.1 | loop fusion | flops 19922944 | bytes 16777216 | tf_op jit(solution)/shard_map/while/body/eval_jaxpr/jit(_where)/select_n | solution.py:16
  82.4 0.0 copy-done
  82.4 2.3 %fusion.12 = f32[3,512]{1,0:T(4,128)S(1)} fusion(f32[512,2048]{1,0:T(8,128)S(1)} %get-tuple-element.181, f32[3,2048]{1,0:T(4,128)S(1)} %get-tuple-element.178, f32[512,2048]{1,0:T(8,128)S(1)} %get-tuple-element.182, f32[3,2048]{1,0:T(4,128)S(1)} %get-tuple-element.177, f32[3,512]{1,0:T(4,128)S(1)} %copy-done), kind=kLoop, calls=%fused_computation.6.clone.1 | loop fusion | flops 15727104 | bytes 8450048 | tf_op jit(solution)/shard_map/while/body/eval_jaxpr/reduce_sum | solution.py:23
  84.7 8.2 %fusion.10 = (f32[512,2048]{1,0:T(8,128)S(1)}, f32[512,2048]{1,0:T(8,128)S(1)}) fusion(f32[3,2048]{1,0:T(4,128)S(1)} %get-tuple-element.177, f32[3,512]{1,0:T(4,128)} %get-tuple-element.203, f32[3,2048]{1,0:T(4,128)S(1)} %get-tuple-element.178), kind=kLoop, calls=%fused_computation.3.clone.1 | loop fusion | flops 13631488 | bytes 8443904 | tf_op jit(solution)/shard_map/while/body/eval_jaxpr/reduce_sum | solution.py:9
  92.9 0.0 copy-start
  92.9 3.6 %fusion.11 = (f32[512,2048]{1,0:T(8,128)S(1)}, f32[512,2048]{1,0:T(8,128)S(1)}) fusion(f32[512,2048]{1,0:T(8,128)S(1)} %get-tuple-element.179, f32[512,2048]{1,0:T(8,128)S(1)} %get-tuple-element.180), kind=kLoop, calls=%fused_computation.11.clone.1 | loop fusion | flops 19922944 | bytes 16777216 | tf_op jit(solution)/shard_map/while/body/eval_jaxpr/jit(_where)/select_n | solution.py:16
  96.5 0.0 copy-done
  96.5 2.3 %fusion.12 = f32[3,512]{1,0:T(4,128)S(1)} fusion(f32[512,2048]{1,0:T(8,128)S(1)} %get-tuple-element.181, f32[3,2048]{1,0:T(4,128)S(1)} %get-tuple-element.178, f32[512,2048]{1,0:T(8,128)S(1)} %get-tuple-element.182, f32[3,2048]{1,0:T(4,128)S(1)} %get-tuple-element.177, f32[3,512]{1,0:T(4,128)S(1)} %copy-done), kind=kLoop, calls=%fused_computation.6.clone.1 | loop fusion | flops 15727104 | bytes 8450048 | tf_op jit(solution)/shard_map/while/body/eval_jaxpr/reduce_sum | solution.py:23
  98.8 0.0 copy-done.1
  98.8 0.6 multiply_reduce_fusion.1
  99.4 31.7 %all-reduce = (f32[]{:T(128)}, f32[]{:T(128)}) all-reduce(f32[]{:T(128)} %get-tuple-element.119, f32[]{:T(128)} %get-tuple-element.118), channel_id=1, replica_groups=mesh['real'=2,'tile'=16] {'tile'}, use_global_device_ids=true, to_apply=%region_1.0 | all-reduce | flops 2 | bytes 16 | tf_op jit(solution)/shard_map/psum | solution.py:31
  132.5 0.6 multiply_reduce_fusion
  133.1 0.0 copy-start.2
  133.1 30.1 %psum.23 = f32[]{:T(128)} all-reduce(f32[]{:T(128)} %get-tuple-element.132), channel_id=1, replica_groups=mesh['real'=2,'tile'=16] {'tile'}, use_global_device_ids=true, to_apply=%region_10.11 | all-reduce | flops 1 | bytes 8 | tf_op jit(solution)/shard_map/psum | solution.py:50
  164.5 0.0 copy-done.3
  164.5 0.6 multiply_add_fusion
  165.1 0.0 copy-done.2
  (9 shorter events, 0.1 us)
Async XLA Ops:
  42.4 56.5 %copy-start.1 = (f32[3,512]{1,0:T(4,128)S(1)}, f32[3,512]{1,0:T(4,128)}, u32[]{:S(2)}) copy-start(f32[3,512]{1,0:T(4,128)} %param.6) | copy-start | bytes 18436
  42.4 122.2 %copy-start.3 = (f32[3,512]{1,0:T(4,128)S(1)}, f32[3,512]{1,0:T(4,128)}, u32[]{:S(2)}) copy-start(f32[3,512]{1,0:T(4,128)} %param.7) | copy-start | bytes 18436
  50.6 3.6 %copy-start = (f32[3,512]{1,0:T(4,128)S(1)}, f32[3,512]{1,0:T(4,128)}, u32[]{:S(2)}) copy-start(f32[3,512]{1,0:T(4,128)} %get-tuple-element.203) | copy-start | bytes 18436 | tf_op jit(solution)/shard_map/while
  64.7 3.6 %copy-start = (f32[3,512]{1,0:T(4,128)S(1)}, f32[3,512]{1,0:T(4,128)}, u32[]{:S(2)}) copy-start(f32[3,512]{1,0:T(4,128)} %get-tuple-element.203) | copy-start | bytes 18436 | tf_op jit(solution)/shard_map/while
  78.8 3.6 %copy-start = (f32[3,512]{1,0:T(4,128)S(1)}, f32[3,512]{1,0:T(4,128)}, u32[]{:S(2)}) copy-start(f32[3,512]{1,0:T(4,128)} %get-tuple-element.203) | copy-start | bytes 18436 | tf_op jit(solution)/shard_map/while
  92.9 3.6 %copy-start = (f32[3,512]{1,0:T(4,128)S(1)}, f32[3,512]{1,0:T(4,128)}, u32[]{:S(2)}) copy-start(f32[3,512]{1,0:T(4,128)} %get-tuple-element.203) | copy-start | bytes 18436 | tf_op jit(solution)/shard_map/while
  133.1 32.1 %copy-start.2 = (f32[3,512]{1,0:T(4,128)}, f32[3,512]{1,0:T(4,128)S(1)}, u32[]{:S(2)}) copy-start(f32[3,512]{1,0:T(4,128)S(1)} %get-tuple-element.133) | copy-start | bytes 18436
where the time goes:
time: 166 us; the launch traced here: 165 us
  blocking collectives  104 us (63%)
  other arithmetic  57.9 us (35%)
  between operations  3.34 us (2%)
    reduce_sum x4, other arithmetic, pair_terms(): squared = jnp.sum(separation * separation, axis=0)  32.7 us
    psum x1, blocking collectives, shards(): old_norm = lax.psum(jnp.sum(residual * residual), 'tile')  31.7 us
    psum x1, blocking collectives, shards(): new_norm = lax.psum(jnp.sum(new_residual * new_residual), 'tile')  30.1 us
    all_gather x1, blocking collectives, shards(): col_pos = lax.all_gather(positions, 'tile', axis=1, tiled=True)  23.7 us
    all_gather x1, blocking collectives, shards(): col_forces = lax.all_gather(residual, 'tile', axis=1, tiled=True)  18 us
    select_n x4, other arithmetic, pair_terms(): scalar_part = jnp.where(touching, 1.0 - 9.0 / 32.0 * radius, far_scalar)  14.3 us
    reduce_sum x4, other arithmetic, toward_rows(): jnp.sum(scalar_part[None] * col_forces[:, None, :] + (tensor_part * proje...  9.06 us

commit v1 on v0

v1 whole, which is shorter than its diff:
```python
import functools

import jax
import jax.numpy as jnp
from jax import lax
from jax.experimental import pallas as pl
from jax.experimental.pallas import tpu as pltpu
from jax.sharding import PartitionSpec as P

LANES = 128
ROWS = 8


def pair_kernel(diagonal, rows_ref, blobs_ref, base_ref, out_ref):
    cols = blobs_ref.shape[1] // LANES
    own = rows_ref.shape[1]

    def row_tile(tile, carry):
        at = pl.ds(pl.multiple_of(tile * ROWS, ROWS), ROWS)
        px, py, pz = rows_ref[0, at, :], rows_ref[1, at, :], rows_ref[2, at, :]

        def col_tile(col, acc):
            lane = pl.ds(pl.multiple_of(col * LANES, LANES), LANES)
            qx, qy, qz = blobs_ref[0:1, lane], blobs_ref[1:2, lane], blobs_ref[2:3, lane]
            fx, fy, fz = blobs_ref[4:5, lane], blobs_ref[5:6, lane], blobs_ref[6:7, lane]
            dx, dy, dz = px - qx, py - qy, pz - qz
            squared = dx * dx + dy * dy + dz * dz
            if diagonal:
                inverse = lax.rsqrt(jnp.maximum(squared, 0.25))
            else:
                inverse = lax.rsqrt(squared)
            radius = squared * inverse
            inverse_sq = inverse * inverse
            cube = inverse * inverse_sq
            touching = squared < 4.0
            scalar = jnp.where(touching, 1.0 - (9.0 / 32.0) * radius, 0.75 * inverse + 0.5 * cube)
            tensor = jnp.where(touching, (3.0 / 32.0) * inverse, cube * (0.75 - 1.5 * inverse_sq))
            weight = tensor * (dx * fx + dy * fy + dz * fz)
            ax, ay, az = acc
            return (
                ax + (scalar * fx + weight * dx),
                ay + (scalar * fy + weight * dy),
                az + (scalar * fz + weight * dz),
            )

        acc = tuple(base_ref[k, at, :] for k in range(3))
        acc = lax.fori_loop(0, cols, col_tile, acc, unroll=4)
        for k in range(3):
            out_ref[k, at, :] = acc[k]
        return carry

    lax.fori_loop(0, own // ROWS, row_tile, 0)


def add_pairs(diagonal, rows, blobs, base):
    own = rows.shape[1]
    pairs = own * blobs.shape[1]
    return pl.pallas_call(
        functools.partial(pair_kernel, diagonal),
        out_shape=jax.ShapeDtypeStruct(base.shape, jnp.float32),
        in_specs=[pl.BlockSpec(memory_space=pltpu.VMEM)] * 3,
        out_specs=pl.BlockSpec(memory_space=pltpu.VMEM),
        input_output_aliases={2: 0},
        compiler_params=pltpu.CompilerParams(vmem_limit_bytes=4 << 20),
        cost_estimate=pl.CostEstimate(flops=45 * pairs, bytes_accessed=4 * 2 * base.size, transcendentals=pairs),
    )(rows, blobs, base)


def strides(devices):
    out, step = [], devices // 2
    while step:
        out.append(step)
        step //= 2
    return out


def swap(value, devices, step):
    return lax.ppermute(value, "tile", [(i, i ^ step) for i in range(devices)])


def shards(devices, positions, residual, iterate):
    own = positions.shape[1]
    gap = jnp.zeros((1, own), jnp.float32)
    held = jnp.concatenate([positions, gap, residual, gap], axis=0)
    rows = jnp.broadcast_to(positions[:, :, None], (3, own, LANES))
    applied = jnp.zeros((3, own, LANES), jnp.float32)
    fresh, diagonal = held, True
    for step in strides(devices):
        arrived = swap(held, devices, step)
        applied = add_pairs(diagonal, rows, fresh, applied)
        applied, arrived = lax.optimization_barrier((applied, arrived))
        held = jnp.concatenate([held, arrived], axis=1)
        fresh, diagonal = arrived, False
    applied = add_pairs(diagonal, rows, fresh, applied)
    image = jnp.sum(applied, axis=2)
    sums = jnp.stack([jnp.sum(residual * residual), jnp.sum(residual * image), jnp.sum(image * image)])
    for step in strides(devices):
        sums = sums + swap(sums, devices, step)
    old_norm, curvature, image_norm = sums[0], sums[1], sums[2]
    step_size = old_norm / curvature
    new_norm = old_norm - 2.0 * step_size * curvature + step_size * step_size * image_norm
    new_residual = residual - step_size * image
    new_iterate = iterate + step_size * residual
    new_direction = new_residual + new_norm / old_norm * residual
    return (new_iterate, new_residual, new_direction)


def solution(mesh):
    spec = P("real", "tile")
    return jax.shard_map(
        functools.partial(shards, mesh.shape["tile"]),
        mesh=mesh,
        in_specs=(spec, spec, spec),
        out_specs=(spec, spec, spec),
        check_vma=False,
    )
```

time: 166 us -> 68.3 us (0.41)
  blocking collectives: 104 us -> 0 us
  other arithmetic: 57.9 us -> 8.38 us
  Pallas kernels: 0 us -> 33.4 us
  starting transfers between devices: 0 us -> 11.7 us
  waiting for transfers between devices: 0 us -> 8.81 us
    psum x2 -> x0, blocking collectives: 61.8 us -> none  [the longest x1 31.7 us: shards(): old_norm = lax.psum(jnp.sum(residual * residual), 'tile')]
    reduce_sum x10 -> x2, other arithmetic: 42.9 us -> 0.9 us  [the longest x1 0.61 us: shards(): jnp.sum(residual * residual)]
    all_gather x2 -> x0, blocking collectives: 41.7 us -> none  [the longest x1 23.7 us: shards(): col_pos = lax.all_gather(positions, 'tile', axis=1, tiled=True)]
    pallas_call x0 -> x5, Pallas kernels: none -> 33.4 us  [add_pairs(): pl.pallas_call(functools.partial(pair_kernel, diagonal), out_shape=jax.Sh...]
    select_n x4 -> x0, other arithmetic: 14.3 us -> none  [pair_terms(): scalar_part = jnp.where(touching, 1.0 - 9.0 / 32.0 * radius, far_scalar)]
    ppermute x0 -> x8, starting transfers between devices: none -> 11.7 us  [swap(): return lax.ppermute(value, 'tile', [(i, i ^ step) for i in range(devices)])]
    ppermute x0 -> x8, waiting for transfers between devices: none -> 8.81 us  [swap(): return lax.ppermute(value, 'tile', [(i, i ^ step) for i in range(devices)])]
    add x4, other arithmetic: 0.05 us -> 4.04 us  [shards(): sums = sums + swap(sums, devices, step)]
  transfers between devices with their start and end apart: 0 -> 8, of which waited for: 0 -> 5; matrix products, arithmetic and copies ran while one was open for 0% -> 0% of each run, Pallas kernels for 0% -> 25%
where the time goes in v1:
time: 68.3 us; the launch traced here: 68 us
  Pallas kernels  33.4 us (49%)
  starting transfers between devices  11.7 us (17%)
  waiting for transfers between devices  8.81 us (13%)
  other arithmetic  8.38 us (12%)
  between operations  4.77 us (7%)
  local copies, waits for them, and re-layouts  0.92 us (1%)
    pallas_call x5, Pallas kernels, add_pairs(): pl.pallas_call(functools.partial(pair_kernel, diagonal), out_shape=jax.Sh...  33.4 us
    ppermute x8, starting transfers between devices, swap(): return lax.ppermute(value, 'tile', [(i, i ^ step) for i in range(devices)])  11.7 us
    ppermute x8, waiting for transfers between devices, swap(): return lax.ppermute(value, 'tile', [(i, i ^ step) for i in range(devices)])  8.81 us
    add x4, other arithmetic, shards(): sums = sums + swap(sums, devices, step)  4.04 us
    another operation x1, other arithmetic, shards(): jnp.stack([jnp.sum(residual * residual), jnp.sum(residual * image), jnp.s...  2.01 us
  transfers between devices with their start and end apart: 8, of which 5 were waited for; matrix products, arithmetic and copies ran while one was open for 0% of the time, Pallas kernels for 25%

profile of v1, /device:TPU:0, one launch (start us, length us, event | category | flops | bytes accessed | tf_op | source)
XLA Modules:
  0.0 68.0 jit_solution(9442268448876720082)
XLA Ops:
  0.6 0.0 copy-start.1
  0.7 0.8 %pad_maximum_fusion.3.blobs_ref = f32[8,512]{1,0:T(8,128)S(1)} fusion(f32[1,512]{1,0:T(1,128)S(1)} %broadcast_in_dim.13, f32[3,512]{1,0:T(4,128)} %param.4, f32[3,512]{1,0:T(4,128)} %param.3), kind=kLoop, calls=%fused_computation.3 | loop fusion | flops 12288 | bytes 30720 | tf_op jit(solution)/shard_map/concatenate | solution.py:84
  1.4 4.1 %collective-permute-start = (f32[8,512]{1,0:T(8,128)S(1)}, f32[8,512]{1,0:T(8,128)S(1)}, u32[]{:S(2)}, u32[]{:S(2)}) collective-permute-start(f32[8,512]{1,0:T(8,128)S(1)} %pad_maximum_fusion.3.blobs_ref), channel_id=1, source_target_pairs={{0,8},{1,9},{2,10},{3,11},{4,12},{5,13},{6,14},{7,15},{8,0},{9,1},... | collective-permute-start | bytes 49160 | tf_op jit(solution)/shard_map/ppermute | solution.py:78
  5.6 0.0 copy-done.1
  5.6 0.3 broadcast_in_dim.12.rows_ref
  5.8 0.1 broadcast_in_dim.14.base_ref
  5.9 0.0 copy-start
  5.9 2.1 %shard_map.58.base_ref = f32[3,512,128]{2,1,0:T(8,128)S(1)} custom-call(f32[3,512,128]{2,1,0:T(8,128)S(1)} %broadcast_in_dim.12.rows_ref, f32[8,512]{1,0:T(8,128)S(1)} %pad_maximum_fusion.3.blobs_ref, f32[3,512,128]{2,1,0:T(8,128)S(1)} %broadcast_in_dim.14.base_ref), custom_call_target="tpu_custom_call", output_to_operand_aliasing={{}: (2, {})} | custom-call | flops 11796480 | bytes 1572864 | tf_op jit(solution)/shard_map/pallas_call | solution.py:58
  8.0 0.0 collective-permute-done.blobs_ref
  8.0 0.0 copy-done
  8.0 1.6 %collective-permute-start.1 = (f32[8,1024]{1,0:T(8,128)S(1)}, f32[8,1024]{1,0:T(8,128)S(1)}, u32[]{:S(2)}, u32[]{:S(2)}) collective-permute-start(f32[8,1024]{1,0:T(8,128)S(1)} %pad_maximum_fusion.2), channel_id=1, source_target_pairs={{0,4},{1,5},{2,6},{3,7},{4,0},{5,1},{6,2},{7,3},{8,12},{9,13},{10,... | collective-permute-start | bytes 98312 | tf_op jit(solution)/shard_map/ppermute | solution.py:78
  9.6 2.0 %shard_map.59.base_ref = f32[3,512,128]{2,1,0:T(8,128)S(1)} custom-call(f32[3,512,128]{2,1,0:T(8,128)S(1)} %broadcast_in_dim.12.rows_ref, f32[8,512]{1,0:T(8,128)S(1)} %collective-permute-done.blobs_ref, f32[3,512,128]{2,1,0:T(8,128)S(1)} %shard_map.58.base_ref), custom_call_target="tpu_custom_call", output_to_operand_aliasing={{}: (2, {})} | custom-call | flops 11796480 | bytes 1572864 | tf_op jit(solution)/shard_map/pallas_call | solution.py:58
  11.6 0.3 collective-permute-done.1.blobs_ref
  12.0 1.6 %collective-permute-start.2 = (f32[8,2048]{1,0:T(8,128)S(1)}, f32[8,2048]{1,0:T(8,128)S(1)}, u32[]{:S(2)}, u32[]{:S(2)}) collective-permute-start(f32[8,2048]{1,0:T(8,128)S(1)} %pad_maximum_fusion.1), channel_id=1, source_target_pairs={{0,2},{1,3},{2,0},{3,1},{4,6},{5,7},{6,4},{7,5},{8,10},{9,11},{10,... | collective-permute-start | bytes 196616 | tf_op jit(solution)/shard_map/ppermute | solution.py:78
  13.6 4.5 %shard_map.60.base_ref = f32[3,512,128]{2,1,0:T(8,128)S(1)} custom-call(f32[3,512,128]{2,1,0:T(8,128)S(1)} %broadcast_in_dim.12.rows_ref, f32[8,1024]{1,0:T(8,128)S(1)} %collective-permute-done.1.blobs_ref, f32[3,512,128]{2,1,0:T(8,128)S(1)} %shard_map.59.base_ref), custom_call_target="tpu_custom_call", output_to_operand_aliasing={{}: (2, {})} | custom-call | flops 23592960 | bytes 1572864 | tf_op jit(solution)/shard_map/pallas_call | solution.py:58
  18.1 0.0 collective-permute-done.2.blobs_ref
  18.1 0.1 collective-permute-start.3
  18.2 8.5 %shard_map.61.base_ref = f32[3,512,128]{2,1,0:T(8,128)S(1)} custom-call(f32[3,512,128]{2,1,0:T(8,128)S(1)} %broadcast_in_dim.12.rows_ref, f32[8,2048]{1,0:T(8,128)S(1)} %collective-permute-done.2.blobs_ref, f32[3,512,128]{2,1,0:T(8,128)S(1)} %shard_map.60.base_ref), custom_call_target="tpu_custom_call", output_to_operand_aliasing={{}: (2, {})} | custom-call | flops 47185920 | bytes 1572864 | tf_op jit(solution)/shard_map/pallas_call | solution.py:58
  26.6 0.0 collective-permute-done.3.blobs_ref
  26.7 16.4 %shard_map.62 = f32[3,512,128]{2,1,0:T(8,128)S(1)} custom-call(f32[3,512,128]{2,1,0:T(8,128)S(1)} %broadcast_in_dim.12.rows_ref, f32[8,4096]{1,0:T(8,128)S(1)} %collective-permute-done.3.blobs_ref, f32[3,512,128]{2,1,0:T(8,128)S(1)} %shard_map.61.base_ref), custom_call_target="tpu_custom_call", output_to_operand_aliasing={{}: (2, {})} | custom-call | flops 94371840 | bytes 1572864 | tf_op jit(solution)/shard_map/pallas_call | solution.py:58
  43.1 0.3 reduce_sum.37
  43.4 0.6 multiply_reduce_fusion.2
  44.0 2.0 %pad_maximum_fusion.4 = f32[3]{0:T(128)S(1)} fusion(f32[1]{0:T(128)} %bitcast.2, f32[1]{0:T(128)} %bitcast.1, f32[1]{0:T(128)} %bitcast), kind=kLoop, calls=%fused_computation.10 | loop fusion | flops 6 | bytes 24 | tf_op jit(solution)/shard_map/stack | solution.py:96
  46.0 2.2 %collective-permute-start.4 = (f32[3]{0:T(128)S(1)}, f32[3]{0:T(128)S(1)}, u32[]{:S(2)}, u32[]{:S(2)}) collective-permute-start(f32[3]{0:T(128)S(1)} %pad_maximum_fusion.4), channel_id=1, source_target_pairs={{0,8},{1,9},{2,10},{3,11},{4,12},{5,13},{6,14},{7,15},{8,0},{9,1},... | collective-permute-start | bytes 44 | tf_op jit(solution)/shard_map/ppermute | solution.py:78
  48.2 2.2 %collective-permute-done.4 = f32[3]{0:T(128)S(1)} collective-permute-done((f32[3]{0:T(128)S(1)}, f32[3]{0:T(128)S(1)}, u32[]{:S(2)}, u32[]{:S(2)}) %collective-permute-start.4) | collective-permute-done | bytes 44 | tf_op jit(solution)/shard_map/ppermute | solution.py:78
  50.5 2.0 %fusion.1 = f32[3]{0:T(128)S(1)} fusion(f32[3]{0:T(128)S(1)} %collective-permute-done.4, f32[1]{0:T(128)} %bitcast.2, f32[1]{0:T(128)} %bitcast.1, f32[1]{0:T(128)} %bitcast), kind=kLoop, calls=%fused_computation.12 | loop fusion | flops 9 | bytes 36 | tf_op jit(solution)/shard_map/add | solution.py:98
  52.5 1.6 %collective-permute-start.5 = (f32[3]{0:T(128)S(1)}, f32[3]{0:T(128)S(1)}, u32[]{:S(2)}, u32[]{:S(2)}) collective-permute-start(f32[3]{0:T(128)S(1)} %fusion.1), channel_id=1, source_target_pairs={{0,4},{1,5},{2,6},{3,7},{4,0},{5,1},{6,2},{7,3},{8,12},{9,13},{10,... | collective-permute-start | bytes 44 | tf_op jit(solution)/shard_map/ppermute | solution.py:78
  54.1 2.0 %collective-permute-done.5 = f32[3]{0:T(128)S(1)} collective-permute-done((f32[3]{0:T(128)S(1)}, f32[3]{0:T(128)S(1)}, u32[]{:S(2)}, u32[]{:S(2)}) %collective-permute-start.5) | collective-permute-done | bytes 44 | tf_op jit(solution)/shard_map/ppermute | solution.py:78
  56.0 2.0 %fusion.2 = f32[3]{0:T(128)S(1)} fusion(f32[3]{0:T(128)S(1)} %collective-permute-done.5, f32[3]{0:T(128)S(1)} %collective-permute-done.4, f32[1]{0:T(128)} %bitcast.2, f32[1]{0:T(128)} %bitcast.1, f32[1]{0:T(128)} %bitcast), kind=kLoop, calls=%fused_computation.13 | loop fusion | flops 12 | bytes 48 | tf_op jit(solution)/shard_map/add | solution.py:98
  58.1 0.5 collective-permute-start.6
  58.6 3.1 %collective-permute-done.6 = f32[3]{0:T(128)S(1)} collective-permute-done((f32[3]{0:T(128)S(1)}, f32[3]{0:T(128)S(1)}, u32[]{:S(2)}, u32[]{:S(2)}) %collective-permute-start.6) | collective-permute-done | bytes 44 | tf_op jit(solution)/shard_map/ppermute | solution.py:78
  61.6 0.0 collective-permute-start.7
  61.6 1.2 %collective-permute-done.7 = f32[3]{0:T(128)S(1)} collective-permute-done((f32[3]{0:T(128)S(1)}, f32[3]{0:T(128)S(1)}, u32[]{:S(2)}, u32[]{:S(2)}) %collective-permute-start.7) | collective-permute-done | bytes 44 | tf_op jit(solution)/shard_map/ppermute | solution.py:78
  62.8 0.6 fusion
  64.7 0.0 copy-start.2
  67.4 0.0 copy-done.2
  67.4 0.6 multiply_add_fusion
  (6 shorter events, 0.1 us)
Async XLA Ops:
  0.6 4.9 %copy-start.1 = (f32[3,512]{1,0:T(4,128)S(1)}, f32[3,512]{1,0:T(4,128)}, u32[]{:S(2)}) copy-start(f32[3,512]{1,0:T(4,128)} %param.3) | copy-start | bytes 18436
  1.4 6.5 %collective-permute-start = (f32[8,512]{1,0:T(8,128)S(1)}, f32[8,512]{1,0:T(8,128)S(1)}, u32[]{:S(2)}, u32[]{:S(2)}) collective-permute-start(f32[8,512]{1,0:T(8,128)S(1)} %pad_maximum_fusion.3.blobs_ref), channel_id=1, source_target_pairs={{0,8},{1,9},{2,10},{3,11},{4,12},{5,13},{6,14},{7,15},{8,0},{9,1},... | collective-permute-start | bytes 49160 | tf_op jit(solution)/shard_map/ppermute | solution.py:78
  5.9 2.1 %copy-start = (f32[3,512]{1,0:T(4,128)S(1)}, f32[3,512]{1,0:T(4,128)}, u32[]{:S(2)}) copy-start(f32[3,512]{1,0:T(4,128)} %param.4) | copy-start | bytes 18436
  8.0 4.0 %collective-permute-start.1 = (f32[8,1024]{1,0:T(8,128)S(1)}, f32[8,1024]{1,0:T(8,128)S(1)}, u32[]{:S(2)}, u32[]{:S(2)}) collective-permute-start(f32[8,1024]{1,0:T(8,128)S(1)} %pad_maximum_fusion.2), channel_id=1, source_target_pairs={{0,4},{1,5},{2,6},{3,7},{4,0},{5,1},{6,2},{7,3},{8,12},{9,13},{10,... | collective-permute-start | bytes 98312 | tf_op jit(solution)/shard_map/ppermute | solution.py:78
  12.0 6.1 %collective-permute-start.2 = (f32[8,2048]{1,0:T(8,128)S(1)}, f32[8,2048]{1,0:T(8,128)S(1)}, u32[]{:S(2)}, u32[]{:S(2)}) collective-permute-start(f32[8,2048]{1,0:T(8,128)S(1)} %pad_maximum_fusion.1), channel_id=1, source_target_pairs={{0,2},{1,3},{2,0},{3,1},{4,6},{5,7},{6,4},{7,5},{8,10},{9,11},{10,... | collective-permute-start | bytes 196616 | tf_op jit(solution)/shard_map/ppermute | solution.py:78
  18.1 8.5 %collective-permute-start.3 = (f32[8,4096]{1,0:T(8,128)S(1)}, f32[8,4096]{1,0:T(8,128)S(1)}, u32[]{:S(2)}, u32[]{:S(2)}) collective-permute-start(f32[8,4096]{1,0:T(8,128)S(1)} %pad_maximum_fusion), channel_id=1, source_target_pairs={{0,1},{1,0},{2,3},{3,2},{4,5},{5,4},{6,7},{7,6},{8,9},{9,8},{10,11... | collective-permute-start | bytes 393224 | tf_op jit(solution)/shard_map/ppermute | solution.py:78
  46.0 4.5 %collective-permute-start.4 = (f32[3]{0:T(128)S(1)}, f32[3]{0:T(128)S(1)}, u32[]{:S(2)}, u32[]{:S(2)}) collective-permute-start(f32[3]{0:T(128)S(1)} %pad_maximum_fusion.4), channel_id=1, source_target_pairs={{0,8},{1,9},{2,10},{3,11},{4,12},{5,13},{6,14},{7,15},{8,0},{9,1},... | collective-permute-start | bytes 44 | tf_op jit(solution)/shard_map/ppermute | solution.py:78
  52.5 3.6 %collective-permute-start.5 = (f32[3]{0:T(128)S(1)}, f32[3]{0:T(128)S(1)}, u32[]{:S(2)}, u32[]{:S(2)}) collective-permute-start(f32[3]{0:T(128)S(1)} %fusion.1), channel_id=1, source_target_pairs={{0,4},{1,5},{2,6},{3,7},{4,0},{5,1},{6,2},{7,3},{8,12},{9,13},{10,... | collective-permute-start | bytes 44 | tf_op jit(solution)/shard_map/ppermute | solution.py:78
  58.1 3.6 %collective-permute-start.6 = (f32[3]{0:T(128)S(1)}, f32[3]{0:T(128)S(1)}, u32[]{:S(2)}, u32[]{:S(2)}) collective-permute-start(f32[3]{0:T(128)S(1)} %fusion.2), channel_id=1, source_target_pairs={{0,2},{1,3},{2,0},{3,1},{4,6},{5,7},{6,4},{7,5},{8,10},{9,11},{10,... | collective-permute-start | bytes 44 | tf_op jit(solution)/shard_map/ppermute | solution.py:78
  61.6 1.2 %collective-permute-start.7 = (f32[3]{0:T(128)S(1)}, f32[3]{0:T(128)S(1)}, u32[]{:S(2)}, u32[]{:S(2)}) collective-permute-start(f32[3]{0:T(128)S(1)} %add.23), channel_id=1, source_target_pairs={{0,1},{1,0},{2,3},{3,2},{4,5},{5,4},{6,7},{7,6},{8,9},{9,8},{10,11... | collective-permute-start | bytes 44 | tf_op jit(solution)/shard_map/ppermute | solution.py:78
  64.7 2.7 %copy-start.2 = (f32[3,512]{1,0:T(4,128)S(1)}, f32[3,512]{1,0:T(4,128)}, u32[]{:S(2)}) copy-start(f32[3,512]{1,0:T(4,128)} %param.5) | copy-start | bytes 18436

commit v2 on v1

v2 whole, which is shorter than its diff:
```python
import functools

import jax
import jax.numpy as jnp
from jax import lax
from jax.experimental import pallas as pl
from jax.experimental.pallas import tpu as pltpu
from jax.sharding import PartitionSpec as P

LANES = 128
ROWS = 8
SUB = 128
DEPTH = 128
CENTRE = 64.0
STRETCH = 1.5**0.5
FORCE = 0.75 * STRETCH
NEAR_SQ = 4.0 * 1.5
NEAR_CONST = 1.0 / FORCE
NEAR_SLOPE = 9.0 / (32.0 * STRETCH * FORCE)
NEAR_TENSOR = 1.0 / 36.0
FAR_AWAY = 1e30


def bf16(value):
    return value.astype(jnp.bfloat16).astype(jnp.float32)


def thirds(value):
    high = bf16(value)
    rest = value - high
    middle = bf16(rest)
    return high, middle, bf16(rest - middle)


def row_index(value):
    return lax.broadcasted_iota(jnp.int32, value.shape, 0)


def splits(blobs):
    row = row_index(blobs)
    place = row < 4
    tripled = jnp.where((row >= 4) & (row < 7), 3.0 * blobs, blobs)
    high = jnp.where(place, 0.5 * jnp.round(2.0 * blobs), bf16(tripled))
    rest = tripled - high
    middle = bf16(rest)
    low = bf16(rest - middle)
    return tripled, high, rest, middle, low


def column_features(blobs):
    row = row_index(blobs)
    tripled, high, rest, middle, low = splits(blobs)
    product = jnp.where(row < 4, high * high, tripled * pltpu.roll(blobs, 4, 0))
    p_high, p_middle, p_low = thirds(product)
    e_high, e_middle, e_low = thirds(rest * (2.0 * high + rest))
    zero = jnp.zeros_like(blobs)
    return [
        high, p_high, p_middle, high, high, middle, middle, middle,
        low, low, p_low, e_high, e_middle, e_low, zero, zero,
    ]


def row_features(blobs):
    row = row_index(blobs)
    place = row < 3
    _, high, rest, middle, low = splits(blobs)
    n_high, n_middle, n_low = thirds(jnp.sum(jnp.where(place, high * high, 0.0), axis=0, keepdims=True))
    fine = rest * (2.0 * high + rest)
    m_high, m_middle, m_low = thirds(jnp.sum(jnp.where(place, fine, 0.0), axis=0, keepdims=True))
    zero = jnp.zeros_like(blobs)
    one = jnp.where(place, 1.0, zero)

    def on(base, third, seventh):
        base = jnp.where(row == 3, third, jnp.where(place, base, 0.0))
        return jnp.where(row == 7, seventh, base)

    far = [
        on(-2.0 * high, n_high, n_middle), on(one, n_low, 0.0), one,
        on(-2.0 * middle, m_high, m_middle), on(-2.0 * low, m_low, 0.0),
        on(-2.0 * high, 0.0, 0.0), on(-2.0 * middle, 0.0, 0.0), on(-2.0 * low, 0.0, 0.0),
        on(-2.0 * high, 0.0, 0.0), on(-2.0 * middle, 0.0, 0.0),
        zero, one, one, one, zero, zero,
    ]

    def lift(value):
        return pltpu.roll(jnp.where(place, value, 0.0), 4, 0)

    big, mid, small, minus = lift(high), lift(middle), lift(low), lift(-one)
    along = [
        big, minus, minus, mid, small, big, mid, small,
        big, mid, minus, zero, zero, zero, zero, zero,
    ]
    return far, along


def pair_kernel(diagonal, *refs):
    if diagonal:
        blobs_ref, out_ref, lhs_ref, rhs_ref, even_ref, odd_ref = refs
    else:
        blobs_ref, lhs_ref, base_ref, out_ref, rhs_ref, even_ref, odd_ref = refs
    subs = lhs_ref.shape[0]
    own = subs * SUB
    chunks = blobs_ref.shape[1] // own
    steps = subs * chunks

    if diagonal:
        far, along = row_features(blobs_ref[...])
        far = jnp.concatenate(far, axis=0).T.astype(jnp.bfloat16)
        along = jnp.concatenate(along, axis=0).T.astype(jnp.bfloat16)
        for sub in range(subs):
            lhs_ref[sub, :SUB, :] = far[sub * SUB : (sub + 1) * SUB]
            lhs_ref[sub, SUB:, :] = along[sub * SUB : (sub + 1) * SUB]

    def features(chunk, carry):
        lanes = pl.ds(pl.multiple_of(chunk * own, own), own)
        groups = column_features(blobs_ref[:, lanes])
        for pair in range(DEPTH // 16):
            both = jnp.concatenate(groups[2 * pair : 2 * pair + 2], axis=0)
            rhs_ref[16 * pair : 16 * pair + 16, lanes] = both.astype(jnp.bfloat16)
        return carry

    lax.fori_loop(0, chunks, features, 0)

    def products(step, into_ref):
        lanes = pl.ds(pl.multiple_of(step // subs * own, own), own)
        into_ref[...] = jnp.dot(lhs_ref[step % subs], rhs_ref[:, lanes], preferred_element_type=jnp.float32)

    def add_step(step, from_ref):
        first_row = pl.multiple_of(step % subs * SUB, SUB)
        first_lane = pl.multiple_of(step // subs * own, own)
        source = out_ref if diagonal else None
        columns = []
        for col in range(own // LANES):
            lanes = pl.ds(first_lane + col * LANES, LANES)
            columns.append([jnp.broadcast_to(blobs_ref[k : k + 1, lanes], (ROWS, LANES)) for k in (0, 1, 2, 4, 5, 6)])
        for tile in range(SUB // ROWS):
            at = pl.ds(first_row + tile * ROWS, ROWS)
            acc = [out_ref[k, at, :] for k in range(4)]
            for col in range(own // LANES):
                here = slice(tile * ROWS, (tile + 1) * ROWS)
                there = slice(SUB + tile * ROWS, SUB + (tile + 1) * ROWS)
                lanes = slice(col * LANES, (col + 1) * LANES)
                squared, projected = from_ref[here, lanes], from_ref[there, lanes]
                if diagonal:
                    i = lax.broadcasted_iota(jnp.int32, (ROWS, LANES), 0) + (first_row + tile * ROWS)
                    j = lax.broadcasted_iota(jnp.int32, (ROWS, LANES), 1) + col * LANES
                    squared = jnp.where(i == j, FAR_AWAY, squared)
                inverse = lax.rsqrt(squared)
                inverse_sq = inverse * inverse
                cube = inverse * inverse_sq
                near = squared < NEAR_SQ
                scalar = jnp.where(near, NEAR_CONST - NEAR_SLOPE * (squared * inverse), inverse + cube)
                tensor = jnp.where(near, NEAR_TENSOR * inverse, cube * (1.0 / 3.0 - inverse_sq))
                weight = tensor * projected
                x, y, z, fx, fy, fz = columns[col]
                acc[0] = acc[0] + (scalar * fx - weight * x)
                acc[1] = acc[1] + (scalar * fy - weight * y)
                acc[2] = acc[2] + (scalar * fz - weight * z)
                acc[3] = acc[3] + weight
            for k in range(4):
                out_ref[k, at, :] = acc[k]

    out_ref[...] = jnp.zeros_like(out_ref) if diagonal else base_ref[...]
    products(0, even_ref)

    def two_steps(turn, carry):
        step = 2 * turn
        products(step + 1, odd_ref)
        add_step(step, even_ref)
        products(jnp.minimum(step + 2, steps - 1), even_ref)
        add_step(step + 1, odd_ref)
        return carry

    lax.fori_loop(0, steps // 2, two_steps, 0)


def pair_call(blobs, lhs=None, base=None):
    diagonal = lhs is None
    own = blobs.shape[1] if diagonal else lhs.shape[0] * SUB
    vmem = pl.BlockSpec(memory_space=pltpu.VMEM)
    sums = jax.ShapeDtypeStruct((4, own, LANES), jnp.float32)
    rows = jax.ShapeDtypeStruct((own // SUB, 2 * SUB, DEPTH), jnp.bfloat16)
    pairs = own * blobs.shape[1]
    return pl.pallas_call(
        functools.partial(pair_kernel, diagonal),
        out_shape=(sums, rows) if diagonal else sums,
        in_specs=[vmem] * (1 if diagonal else 3),
        out_specs=(vmem, vmem) if diagonal else vmem,
        scratch_shapes=[
            pltpu.VMEM((DEPTH, blobs.shape[1]), jnp.bfloat16),
            pltpu.VMEM((2 * SUB, own), jnp.float32),
            pltpu.VMEM((2 * SUB, own), jnp.float32),
        ],
        input_output_aliases={} if diagonal else {2: 0},
        compiler_params=pltpu.CompilerParams(vmem_limit_bytes=16 << 20),
        cost_estimate=pl.CostEstimate(flops=45 * pairs, bytes_accessed=32 * blobs.shape[1], transcendentals=pairs),
    )(*([blobs] if diagonal else [blobs, lhs, base]))


def finish_kernel(sums_ref, blobs_ref, residual_ref, image_ref, norms_ref):
    ones = jnp.ones((ROWS, LANES), jnp.float32)

    def total(k):
        added = lax.dot_general(
            ones, sums_ref[k], (((1,), (1,)), ((), ())), precision=lax.Precision.HIGHEST, preferred_element_type=jnp.float32
        )
        return added[0:1, :]

    weight = total(3)
    for k in range(3):
        image_ref[k : k + 1, :] = residual_ref[k : k + 1, :] + (total(k) + weight * blobs_ref[k : k + 1, :])
    image, residual = image_ref[...], residual_ref[...]

    def fold(value):
        value = jnp.sum(value, axis=0, keepdims=True)
        return sum(value[:, lane : lane + LANES] for lane in range(0, value.shape[1], LANES))

    norms_ref[...] = jnp.zeros_like(norms_ref)
    norms_ref[0:1, :] = fold(residual * residual)
    norms_ref[1:2, :] = fold(residual * image)
    norms_ref[2:3, :] = fold(image * image)


def finish(sums, blobs, residual):
    vmem = pl.BlockSpec(memory_space=pltpu.VMEM)
    return pl.pallas_call(
        finish_kernel,
        out_shape=(jax.ShapeDtypeStruct(residual.shape, jnp.float32), jax.ShapeDtypeStruct((ROWS, LANES), jnp.float32)),
        in_specs=[vmem] * 3,
        out_specs=(vmem, vmem),
        compiler_params=pltpu.CompilerParams(vmem_limit_bytes=8 << 20),
    )(sums, blobs, residual)


def update_kernel(mine_ref, other_ref, image_ref, residual_ref, iterate_ref, new_iterate_ref, new_residual_ref, new_direction_ref):
    norms = jnp.sum(mine_ref[...] + other_ref[...], axis=1, keepdims=True)
    old_norm, curvature, image_norm = norms[0:1], norms[1:2], norms[2:3]
    step_size = old_norm / curvature
    new_norm = old_norm - 2.0 * step_size * curvature + step_size * step_size * image_norm
    residual = residual_ref[...]
    new_residual = residual - step_size * image_ref[...]
    new_iterate_ref[...] = iterate_ref[...] + step_size * residual
    new_residual_ref[...] = new_residual
    new_direction_ref[...] = new_residual + new_norm / old_norm * residual


def update(mine, other, image, residual, iterate):
    vmem = pl.BlockSpec(memory_space=pltpu.VMEM)
    shape = jax.ShapeDtypeStruct(residual.shape, jnp.float32)
    return pl.pallas_call(
        update_kernel,
        out_shape=(shape,) * 3,
        in_specs=[vmem] * 5,
        out_specs=(vmem,) * 3,
        compiler_params=pltpu.CompilerParams(vmem_limit_bytes=4 << 20),
    )(mine, other, image, residual, iterate)


def strides(devices):
    out, step = [], devices // 2
    while step:
        out.append(step)
        step //= 2
    return out


def swap(value, devices, step):
    return lax.ppermute(value, "tile", [(i, i ^ step) for i in range(devices)])


def shards(devices, positions, residual, iterate):
    one = jnp.ones((1, positions.shape[1]), jnp.float32)
    blobs = jnp.concatenate([STRETCH * (positions - CENTRE), one, FORCE * residual, one], axis=0)
    held, fresh, sums, lhs = blobs, blobs, None, None
    for step in strides(devices):
        arrived = swap(held, devices, step)
        if lhs is None:
            sums, lhs = pair_call(fresh)
        else:
            sums = pair_call(fresh, lhs, sums)
        sums, arrived = lax.optimization_barrier((sums, arrived))
        held = jnp.concatenate([held, arrived], axis=1)
        fresh = arrived
    sums = pair_call(fresh, lhs, sums)
    image, norms = finish(sums, blobs, residual)
    other = jnp.zeros_like(norms)
    for step in strides(devices):
        norms = norms + other
        other = swap(norms, devices, step)
    return update(norms, other, image, residual, iterate)


def solution(mesh):
    spec = P("real", "tile")
    return jax.shard_map(
        functools.partial(shards, mesh.shape["tile"]),
        mesh=mesh,
        in_specs=(spec, spec, spec),
        out_specs=(spec, spec, spec),
        check_vma=False,
    )
```

time: 68.3 us -> 50.2 us (0.73)
  other arithmetic: 8.38 us -> 0.79 us
  Pallas kernels: 33.4 us -> 27.3 us
  between operations: 4.77 us -> 0.76 us
  starting transfers between devices: 11.7 us -> 12.8 us
  local copies, waits for them, and re-layouts: 0.92 us -> 0.01 us
    pallas_call x5 -> x7, Pallas kernels: 33.4 us -> 27.3 us  [the longest x5 25.6 us: pair_call(): pl.pallas_call(functools.partial(pair_kernel, diagonal), out_shape=(sums,...]
    add x5 -> x3, other arithmetic: 4.65 us -> 0.01 us  [shards(): norms = norms + other]
    another operation x1 -> x0, other arithmetic: 2.01 us -> none  [shards(): jnp.stack([jnp.sum(residual * residual), jnp.sum(residual * image), jnp.s...]
    ppermute x8, starting transfers between devices: 11.7 us -> 12.8 us  [swap(): return lax.ppermute(value, 'tile', [(i, i ^ step) for i in range(devices)])]
    reduce_sum x2 -> x0, other arithmetic: 0.9 us -> none  [the longest x1 0.61 us: shards(): jnp.sum(residual * residual)]
    concatenate x1, other arithmetic: 0.78 us -> 0.01 us  [shards(): jnp.concatenate([STRETCH * (positions - CENTRE), one, FORCE * residual, o...]
    mul x0 -> x1, other arithmetic: none -> 0.72 us  [shards(): STRETCH * (positions - CENTRE)]
  transfers between devices with their start and end apart: 8 -> 8, of which waited for: 5 -> 5; matrix products, arithmetic and copies ran while one was open for 0% -> 0% of each run, Pallas kernels for 25% -> 27%
where the time goes in v2:
time: 50.2 us; the launch traced here: 50 us
  Pallas kernels  27.3 us (54%)
  starting transfers between devices  12.8 us (25%)
  waiting for transfers between devices  8.28 us (16%)
  other arithmetic  0.79 us (2%)
  between operations  0.76 us (2%)
    pallas_call x5, Pallas kernels, pair_call(): pl.pallas_call(functools.partial(pair_kernel, diagonal), out_shape=(sums,...  25.6 us
    ppermute x8, starting transfers between devices, swap(): return lax.ppermute(value, 'tile', [(i, i ^ step) for i in range(devices)])  12.8 us
    ppermute x8, waiting for transfers between devices, swap(): return lax.ppermute(value, 'tile', [(i, i ^ step) for i in range(devices)])  8.28 us
  transfers between devices with their start and end apart: 8, of which 5 were waited for; matrix products, arithmetic and copies ran while one was open for 0% of the time, Pallas kernels for 27%

profile of v2, /device:TPU:0, one launch (start us, length us, event | category | flops | bytes accessed | tf_op | source)
XLA Modules:
  0.0 50.0 jit_solution(3044155389690110323)
XLA Ops:
  0.6 0.7 %add_multiply_fusion = (f32[3,512]{1,0:T(4,128)S(1)}, f32[3,512]{1,0:T(4,128)S(1)}) fusion(f32[3,512]{1,0:T(4,128)} %param.3, f32[3,512]{1,0:T(4,128)} %residual_ref.3), kind=kLoop, calls=%fused_computation.4 | loop fusion | flops 4608 | bytes 24576 | tf_op jit(solution)/shard_map/mul | solution.py:273
  1.4 4.1 %collective-permute-start = (f32[8,512]{1,0:T(8,128)S(1)}, f32[8,512]{1,0:T(8,128)S(1)}, u32[]{:S(2)}, u32[]{:S(2)}) collective-permute-start(f32[8,512]{1,0:T(8,128)S(1)} %pad_maximum_fusion.3.refs_0_.blobs_ref), channel_id=1, source_target_pairs={{0,8},{1,9},{2,10},{3,11},{4,12},{5,13},{6,14},{7,15},{8,0},{9,1},... | collective-permute-start | bytes 49160 | tf_op jit(solution)/shard_map/ppermute | solution.py:268
  5.5 1.9 %shard_map.58 = (f32[4,512,128]{2,1,0:T(8,128)S(1)}, bf16[4,256,128]{2,1,0:T(8,128)(2,1)S(1)}) custom-call(f32[8,512]{1,0:T(8,128)S(1)} %pad_maximum_fusion.3.refs_0_.blobs_ref), custom_call_target="tpu_custom_call" | custom-call | flops 11796480 | bytes 16384 | tf_op jit(solution)/shard_map/pallas_call | solution.py:184
  7.4 0.0 collective-permute-done.refs_0_
  7.4 1.8 %collective-permute-start.1 = (f32[8,1024]{1,0:T(8,128)S(1)}, f32[8,1024]{1,0:T(8,128)S(1)}, u32[]{:S(2)}, u32[]{:S(2)}) collective-permute-start(f32[8,1024]{1,0:T(8,128)S(1)} %pad_maximum_fusion.2), channel_id=1, source_target_pairs={{0,4},{1,5},{2,6},{3,7},{4,0},{5,1},{6,2},{7,3},{8,12},{9,13},{10,... | collective-permute-start | bytes 98312 | tf_op jit(solution)/shard_map/ppermute | solution.py:268
  9.2 1.8 %shard_map.59.refs_2_ = f32[4,512,128]{2,1,0:T(8,128)S(1)} custom-call(f32[8,512]{1,0:T(8,128)S(1)} %collective-permute-done.refs_0_, bf16[4,256,128]{2,1,0:T(8,128)(2,1)S(1)} %get-tuple-element.17.refs_1_, f32[4,512,128]{2,1,0:T(8,128)S(1)} %get-tuple-element.18.refs_2_), custom_call_target="tpu_custom_call", output_to_operand_aliasing={{}: (2, {})} | custom-call | flops 11796480 | bytes 16384 | tf_op jit(solution)/shard_map/pallas_call | solution.py:184
  11.0 0.4 collective-permute-done.1.refs_0_
  11.4 1.8 %collective-permute-start.2 = (f32[8,2048]{1,0:T(8,128)S(1)}, f32[8,2048]{1,0:T(8,128)S(1)}, u32[]{:S(2)}, u32[]{:S(2)}) collective-permute-start(f32[8,2048]{1,0:T(8,128)S(1)} %pad_maximum_fusion.1), channel_id=1, source_target_pairs={{0,2},{1,3},{2,0},{3,1},{4,6},{5,7},{6,4},{7,5},{8,10},{9,11},{10,... | collective-permute-start | bytes 196616 | tf_op jit(solution)/shard_map/ppermute | solution.py:268
  13.2 3.3 %shard_map.60.refs_2_ = f32[4,512,128]{2,1,0:T(8,128)S(1)} custom-call(f32[8,1024]{1,0:T(8,128)S(1)} %collective-permute-done.1.refs_0_, bf16[4,256,128]{2,1,0:T(8,128)(2,1)S(1)} %get-tuple-element.17.refs_1_, f32[4,512,128]{2,1,0:T(8,128)S(1)} %shard_map.59.refs_2_), custom_call_target="tpu_custom_call", output_to_operand_aliasing={{}: (2, {})} | custom-call | flops 23592960 | bytes 32768 | tf_op jit(solution)/shard_map/pallas_call | solution.py:184
  16.5 0.0 collective-permute-done.2.refs_0_
  16.6 0.1 collective-permute-start.3
  16.6 6.3 %shard_map.61.refs_2_ = f32[4,512,128]{2,1,0:T(8,128)S(1)} custom-call(f32[8,2048]{1,0:T(8,128)S(1)} %collective-permute-done.2.refs_0_, bf16[4,256,128]{2,1,0:T(8,128)(2,1)S(1)} %get-tuple-element.17.refs_1_, f32[4,512,128]{2,1,0:T(8,128)S(1)} %shard_map.60.refs_2_), custom_call_target="tpu_custom_call", output_to_operand_aliasing={{}: (2, {})} | custom-call | flops 47185920 | bytes 65536 | tf_op jit(solution)/shard_map/pallas_call | solution.py:184
  23.0 0.0 copy-start
  23.0 0.0 collective-permute-done.3.refs_0_
  23.0 12.3 %shard_map.62.sums_ref = f32[4,512,128]{2,1,0:T(8,128)S(1)} custom-call(f32[8,4096]{1,0:T(8,128)S(1)} %collective-permute-done.3.refs_0_, bf16[4,256,128]{2,1,0:T(8,128)(2,1)S(1)} %get-tuple-element.17.refs_1_, f32[4,512,128]{2,1,0:T(8,128)S(1)} %shard_map.61.refs_2_), custom_call_target="tpu_custom_call", output_to_operand_aliasing={{}: (2, {})} | custom-call | flops 94371840 | bytes 131072 | tf_op jit(solution)/shard_map/pallas_call | solution.py:184
  35.3 0.0 copy-done
  35.3 1.0 %shard_map.63 = (f32[3,512]{1,0:T(4,128)S(1)}, f32[8,128]{1,0:T(8,128)S(1)}) custom-call(f32[4,512,128]{2,1,0:T(8,128)S(1)} %shard_map.62.sums_ref, f32[8,512]{1,0:T(8,128)S(1)} %pad_maximum_fusion.3.refs_0_.blobs_ref, f32[3,512]{1,0:T(4,128)S(1)} %copy-done), custom_call_target="tpu_custom_call" | custom-call | tf_op jit(solution)/shard_map/pallas_call | solution.py:226
  36.3 2.6 %collective-permute-start.4 = (f32[8,128]{1,0:T(8,128)S(1)}, f32[8,128]{1,0:T(8,128)S(1)}, u32[]{:S(2)}, u32[]{:S(2)}) collective-permute-start(f32[8,128]{1,0:T(8,128)S(1)} %get-tuple-element.25), channel_id=1, source_target_pairs={{0,8},{1,9},{2,10},{3,11},{4,12},{5,13},{6,14},{7,15},{8,0},{9,1},... | collective-permute-start | bytes 12296 | tf_op jit(solution)/shard_map/ppermute | solution.py:268
  38.9 2.0 %collective-permute-done.4 = f32[8,128]{1,0:T(8,128)S(1)} collective-permute-done((f32[8,128]{1,0:T(8,128)S(1)}, f32[8,128]{1,0:T(8,128)S(1)}, u32[]{:S(2)}, u32[]{:S(2)}) %collective-permute-start.4) | collective-permute-done | bytes 4128 | tf_op jit(solution)/shard_map/ppermute | solution.py:268
  40.8 1.5 %collective-permute-start.5 = (f32[8,128]{1,0:T(8,128)S(1)}, f32[8,128]{1,0:T(8,128)S(1)}, u32[]{:S(2)}, u32[]{:S(2)}) collective-permute-start(f32[8,128]{1,0:T(8,128)S(1)} %add.10), channel_id=1, source_target_pairs={{0,4},{1,5},{2,6},{3,7},{4,0},{5,1},{6,2},{7,3},{8,12},{9,13},{10,... | collective-permute-start | bytes 12296 | tf_op jit(solution)/shard_map/ppermute | solution.py:268
  42.4 2.1 %collective-permute-done.5 = f32[8,128]{1,0:T(8,128)S(1)} collective-permute-done((f32[8,128]{1,0:T(8,128)S(1)}, f32[8,128]{1,0:T(8,128)S(1)}, u32[]{:S(2)}, u32[]{:S(2)}) %collective-permute-start.5) | collective-permute-done | bytes 4128 | tf_op jit(solution)/shard_map/ppermute | solution.py:268
  44.5 0.0 copy-start.1
  44.5 0.9 %collective-permute-start.6 = (f32[8,128]{1,0:T(8,128)S(1)}, f32[8,128]{1,0:T(8,128)S(1)}, u32[]{:S(2)}, u32[]{:S(2)}) collective-permute-start(f32[8,128]{1,0:T(8,128)S(1)} %add.11), channel_id=1, source_target_pairs={{0,2},{1,3},{2,0},{3,1},{4,6},{5,7},{6,4},{7,5},{8,10},{9,11},{10,... | collective-permute-start | bytes 12296 | tf_op jit(solution)/shard_map/ppermute | solution.py:268
  45.4 2.7 %collective-permute-done.6 = f32[8,128]{1,0:T(8,128)S(1)} collective-permute-done((f32[8,128]{1,0:T(8,128)S(1)}, f32[8,128]{1,0:T(8,128)S(1)}, u32[]{:S(2)}, u32[]{:S(2)}) %collective-permute-start.6) | collective-permute-done | bytes 4128 | tf_op jit(solution)/shard_map/ppermute | solution.py:268
  48.1 0.0 collective-permute-start.7
  48.1 1.2 %collective-permute-done.7.other_ref = f32[8,128]{1,0:T(8,128)S(1)} collective-permute-done((f32[8,128]{1,0:T(8,128)S(1)}, f32[8,128]{1,0:T(8,128)S(1)}, u32[]{:S(2)}, u32[]{:S(2)}) %collective-permute-start.7) | collective-permute-done | bytes 4128 | tf_op jit(solution)/shard_map/ppermute | solution.py:268
  49.2 0.0 copy-done.1
  49.2 0.7 %shard_map.64 = (f32[3,512]{1,0:T(4,128)}, f32[3,512]{1,0:T(4,128)}, f32[3,512]{1,0:T(4,128)}) custom-call(f32[8,128]{1,0:T(8,128)S(1)} %add.12.mine_ref, f32[8,128]{1,0:T(8,128)S(1)} %collective-permute-done.7.other_ref, f32[3,512]{1,0:T(4,128)S(1)} %get-tuple-element.26.image_ref, f32[3,512]{1,0:T(4,128)S(1)} %copy-done, f32[3,512]{1,0:T(4,128)S(1)} %copy-done.1), custom_call_target="tpu_custom_call" | custom-call | tf_op jit(solution)/shard_map/pallas_call | solution.py:250
  (8 shorter events, 0.1 us)
Async XLA Ops:
  1.4 6.0 %collective-permute-start = (f32[8,512]{1,0:T(8,128)S(1)}, f32[8,512]{1,0:T(8,128)S(1)}, u32[]{:S(2)}, u32[]{:S(2)}) collective-permute-start(f32[8,512]{1,0:T(8,128)S(1)} %pad_maximum_fusion.3.refs_0_.blobs_ref), channel_id=1, source_target_pairs={{0,8},{1,9},{2,10},{3,11},{4,12},{5,13},{6,14},{7,15},{8,0},{9,1},... | collective-permute-start | bytes 49160 | tf_op jit(solution)/shard_map/ppermute | solution.py:268
  7.4 4.0 %collective-permute-start.1 = (f32[8,1024]{1,0:T(8,128)S(1)}, f32[8,1024]{1,0:T(8,128)S(1)}, u32[]{:S(2)}, u32[]{:S(2)}) collective-permute-start(f32[8,1024]{1,0:T(8,128)S(1)} %pad_maximum_fusion.2), channel_id=1, source_target_pairs={{0,4},{1,5},{2,6},{3,7},{4,0},{5,1},{6,2},{7,3},{8,12},{9,13},{10,... | collective-permute-start | bytes 98312 | tf_op jit(solution)/shard_map/ppermute | solution.py:268
  11.4 5.1 %collective-permute-start.2 = (f32[8,2048]{1,0:T(8,128)S(1)}, f32[8,2048]{1,0:T(8,128)S(1)}, u32[]{:S(2)}, u32[]{:S(2)}) collective-permute-start(f32[8,2048]{1,0:T(8,128)S(1)} %pad_maximum_fusion.1), channel_id=1, source_target_pairs={{0,2},{1,3},{2,0},{3,1},{4,6},{5,7},{6,4},{7,5},{8,10},{9,11},{10,... | collective-permute-start | bytes 196616 | tf_op jit(solution)/shard_map/ppermute | solution.py:268
  16.6 6.4 %collective-permute-start.3 = (f32[8,4096]{1,0:T(8,128)S(1)}, f32[8,4096]{1,0:T(8,128)S(1)}, u32[]{:S(2)}, u32[]{:S(2)}) collective-permute-start(f32[8,4096]{1,0:T(8,128)S(1)} %pad_maximum_fusion), channel_id=1, source_target_pairs={{0,1},{1,0},{2,3},{3,2},{4,5},{5,4},{6,7},{7,6},{8,9},{9,8},{10,11... | collective-permute-start | bytes 393224 | tf_op jit(solution)/shard_map/ppermute | solution.py:268
  23.0 12.3 %copy-start = (f32[3,512]{1,0:T(4,128)S(1)}, f32[3,512]{1,0:T(4,128)}, u32[]{:S(2)}) copy-start(f32[3,512]{1,0:T(4,128)} %residual_ref.3) | copy-start | bytes 18436
  36.3 4.6 %collective-permute-start.4 = (f32[8,128]{1,0:T(8,128)S(1)}, f32[8,128]{1,0:T(8,128)S(1)}, u32[]{:S(2)}, u32[]{:S(2)}) collective-permute-start(f32[8,128]{1,0:T(8,128)S(1)} %get-tuple-element.25), channel_id=1, source_target_pairs={{0,8},{1,9},{2,10},{3,11},{4,12},{5,13},{6,14},{7,15},{8,0},{9,1},... | collective-permute-start | bytes 12296 | tf_op jit(solution)/shard_map/ppermute | solution.py:268
  40.8 3.6 %collective-permute-start.5 = (f32[8,128]{1,0:T(8,128)S(1)}, f32[8,128]{1,0:T(8,128)S(1)}, u32[]{:S(2)}, u32[]{:S(2)}) collective-permute-start(f32[8,128]{1,0:T(8,128)S(1)} %add.10), channel_id=1, source_target_pairs={{0,4},{1,5},{2,6},{3,7},{4,0},{5,1},{6,2},{7,3},{8,12},{9,13},{10,... | collective-permute-start | bytes 12296 | tf_op jit(solution)/shard_map/ppermute | solution.py:268
  44.5 4.8 %copy-start.1 = (f32[3,512]{1,0:T(4,128)S(1)}, f32[3,512]{1,0:T(4,128)}, u32[]{:S(2)}) copy-start(f32[3,512]{1,0:T(4,128)} %iterate_ref.1) | copy-start | bytes 18436
  44.5 3.6 %collective-permute-start.6 = (f32[8,128]{1,0:T(8,128)S(1)}, f32[8,128]{1,0:T(8,128)S(1)}, u32[]{:S(2)}, u32[]{:S(2)}) collective-permute-start(f32[8,128]{1,0:T(8,128)S(1)} %add.11), channel_id=1, source_target_pairs={{0,2},{1,3},{2,0},{3,1},{4,6},{5,7},{6,4},{7,5},{8,10},{9,11},{10,... | collective-permute-start | bytes 12296 | tf_op jit(solution)/shard_map/ppermute | solution.py:268
  48.1 1.2 %collective-permute-start.7 = (f32[8,128]{1,0:T(8,128)S(1)}, f32[8,128]{1,0:T(8,128)S(1)}, u32[]{:S(2)}, u32[]{:S(2)}) collective-permute-start(f32[8,128]{1,0:T(8,128)S(1)} %add.12.mine_ref), channel_id=1, source_target_pairs={{0,1},{1,0},{2,3},{3,2},{4,5},{5,4},{6,7},{7,6},{8,9},{9,8},{10,11... | collective-permute-start | bytes 12296 | tf_op jit(solution)/shard_map/ppermute | solution.py:268
